TPU v7x, 32 devices: a whole 2x2x4 slice. The times are simulated.
32 devices in a mesh: row: 8 (over y, x, core), col: 4 (over z).
Axes of the slice: x: 2, y: 2, z: 4, core: 2. Of those that a mesh axis runs over, the one named last changes fastest.
Arguments:
- right_sides: float32 [8, 8192, 128], P(None, ('row', 'col')), may hold values from -6 to 6
- factor_head: bfloat16 [8, 8192, 4, 1024], P(None, 'row', None, 'col'), may hold values from -0.1875 to 0.1875
- class_head: int32 [8, 8, 4], P(None, 'row'), may hold values from 0 to 2
- scale_head: float32 [8, 8, 4], P(None, 'row'), may hold values from 0.25 to 2
- inverse_head: float32 [4, 1024, 1024], P(None, 'col'), as said below
- factor_tail: bfloat16 [4, 1024, 8, 8192], P(None, 'col', None, 'row'), may hold values from -0.1875 to 0.1875
- class_tail: int32 [4, 8, 8], P(None, None, 'row'), may hold values from 0 to 2
- scale_tail: float32 [4, 8, 8], P(None, None, 'row'), may hold values from 0.25 to 2
- inverse_tail: float32 [4, 1024, 1024], P(None, None, 'col'), as said below
Outputs:
- solved_head: float32 [4, 1024, 128], P(None, 'col')
- solved_tail: float32 [4, 1024, 128], P(None, 'col')
- remainder: float32 [8, 8192, 128], P(None, ('row', 'col'))
Inputs may be any that keep to these rules, and one draw needn't show every extreme that they name: `class_head`: 0, 1, 2 name the float32, bfloat16 and scaled bfloat16 classes. `class_tail`: 0, 1, 2 name the float32, bfloat16 and scaled bfloat16 classes. `inverse_head`: every tile is lower triangular with a diagonal of 1 to 2. `inverse_tail`: every tile is lower triangular with a diagonal of 1 to 2.
All inputs are finite; a program needn't handle non-finite values.
Results may differ from a plain program's by a relative error of at most 0.008.
Values sent between devices are 32-bit elements; how exact they have to be, the bound alone decides.
A program may use at most 128 MiB of HBM per device.

v0:
```python
import jax
import jax.numpy as jnp
from jax import lax
from jax.sharding import PartitionSpec as P


def from_root(block, axis, owner):
    block = jnp.where(lax.axis_index(axis) == owner, block, jnp.zeros_like(block))
    return lax.psum(block, axis)


def tile_terms(stored, classes, scales, solved, form):
    short_piece = solved.astype(jnp.bfloat16)
    exact_term = jnp.einsum(
        form, stored.astype(jnp.float32), solved, precision=lax.Precision.HIGHEST
    )
    short_term = jnp.einsum(form, stored, short_piece, preferred_element_type=jnp.float32)
    classes = classes[:, None, None]
    scales = scales[:, None, None]
    return jnp.where(
        classes == 0, exact_term, jnp.where(classes == 1, short_term, scales * short_term)
    )


def solve_tile(partial_value, right_share, owner_row, invert):
    share_rows = right_share.shape[0]
    placed = lax.dynamic_update_slice_in_dim(
        jnp.zeros(partial_value.shape, jnp.float32),
        right_share,
        lax.axis_index("col") * share_rows,
        0,
    )
    summed = lax.psum(partial_value - placed, "col")
    solved = invert(-summed)
    return from_root(solved, "row", owner_row)


def on_device(
    right_sides,
    factor_head,
    class_head,
    scale_head,
    inverse_head,
    factor_tail,
    class_tail,
    scale_tail,
    inverse_tail,
):
    n_row = lax.axis_size("row")
    slots = right_sides.shape[0]
    ntiles = slots * n_row
    window = inverse_head.shape[0]
    tile_rows = factor_head.shape[1]
    tile_ids = jnp.arange(slots, dtype=jnp.int32) * n_row + lax.axis_index("row")
    updates = jnp.zeros((slots, tile_rows, right_sides.shape[2]), jnp.float32)
    heads = []
    for step in range(window):
        slot_k, row_k = divmod(step, n_row)
        inverse_rows = inverse_head[step]

        def invert_head(value, inverse_rows=inverse_rows):
            return jnp.dot(
                inverse_rows,
                value,
                precision=lax.Precision.HIGHEST,
                preferred_element_type=jnp.float32,
            )

        solved = solve_tile(updates[slot_k], right_sides[slot_k], row_k, invert_head)
        heads.append(solved)
        terms = tile_terms(
            factor_head[:, :, step, :],
            class_head[:, 0, step],
            scale_head[:, 0, step],
            solved,
            "lab,bn->lan",
        )
        active = (tile_ids > step)[:, None, None]
        updates = updates + jnp.where(active, terms, jnp.float32(0.0))
    tails = [None] * window
    for step in range(window):
        target = ntiles - 1 - step
        position = window - 1 - step
        slot_j, row_j = divmod(target, n_row)
        inverse_cols = inverse_tail[position]

        def invert_tail(value, inverse_cols=inverse_cols):
            return jnp.dot(
                inverse_cols.T,
                value,
                precision=lax.Precision.HIGHEST,
                preferred_element_type=jnp.float32,
            )

        solved = solve_tile(updates[slot_j], right_sides[slot_j], row_j, invert_tail)
        tails[position] = solved
        terms = tile_terms(
            factor_tail[position],
            class_tail[position, :, 0],
            scale_tail[position, :, 0],
            solved,
            "alb,an->lbn",
        )
        active = (tile_ids < target)[:, None, None]
        updates = updates + jnp.where(active, terms, jnp.float32(0.0))
    summed = lax.psum_scatter(updates, "col", scatter_dimension=1, tiled=True)
    return (jnp.stack(heads), jnp.stack(tails), right_sides - summed)


def solution(mesh):
    return jax.shard_map(
        on_device,
        mesh=mesh,
        in_specs=(
            P(None, ("row", "col"), None),
            P(None, "row", None, "col"),
            P(None, "row", None),
            P(None, "row", None),
            P(None, "col", None),
            P(None, "col", None, "row"),
            P(None, None, "row"),
            P(None, None, "row"),
            P(None, None, "col"),
        ),
        out_specs=(P(None, "col", None), P(None, "col", None), P(None, ("row", "col"), None)),
        check_vma=False,
    )
```

profile of v0, /device:TPU:0, one launch (start us, length us, event | category | flops | bytes accessed | tf_op | source)
XLA Modules:
  0.0 989.1 jit_solution(2727695291262709679)
XLA Ops:
  7.2 1.6 copy.12
  8.9 0.8 broadcast_subtract_fusion
  9.8 41.2 %fusion.101 = (bf16[8,1024,1,256]{3,2,1,0:T(2,128)(2,1)}, bf16[8,1024,1,256]{3,2,1,0:T(2,128)(2,1)}, bf16[8,1024,1,256]{3,2,1,0:T(2,128)(2,1)}, bf16[8,1024,1,256]{3,2,1,0:T(2,128)(2,1)}) fusion(bf16[8,1024,4,256]{3,2,1,0:T(4,128)(2,1)} %param.10), kind=kLoop, calls=%fused_computation.170 | loop fusion | bytes 33554432 | tf_op jit(solution)/shard_map/slice | solution.py:72
  51.0 1.1 all-reduce.17.cloned.1.call-done
  52.2 3.2 fusion.42
  55.5 55.1 %all-reduce.19.cloned.1.call-done = f32[256,128]{0,1:T(8,128)} async-done(((f32[256,128]{0,1:T(8,128)}), f32[256,128]{0,1:T(8,128)}) %all-reduce.19.cloned.1.call-update) | async-done | bytes 131088 | tf_op jit(solution)/shard_map/psum | solution.py:9
  110.6 7.9 fusion.31
  118.5 1.6 fusion.1
  120.1 2.0 copy-done.17
  122.1 0.9 fusion.65
  123.0 38.1 %all-reduce.21.cloned.1.call-done = f32[1024,128]{0,1:T(8,128)} async-done(((f32[1024,128]{0,1:T(8,128)}), f32[1024,128]{0,1:T(8,128)}) %all-reduce.21.cloned.1.call-update) | async-done | bytes 524304 | tf_op jit(solution)/shard_map/psum | solution.py:33
  161.1 3.2 fusion.41
  164.6 53.3 %all-reduce.23.cloned.1.call-done = f32[256,128]{0,1:T(8,128)} async-done(((f32[256,128]{0,1:T(8,128)}), f32[256,128]{0,1:T(8,128)}) %all-reduce.23.cloned.1.call-update) | async-done | bytes 131088 | tf_op jit(solution)/shard_map/psum | solution.py:9
  217.9 7.8 fusion.32
  225.7 5.0 fusion.4
  230.7 2.0 copy-done.11
  232.7 0.9 fusion.64
  233.6 38.2 %all-reduce.25.cloned.1.call-done = f32[1024,128]{0,1:T(8,128)} async-done(((f32[1024,128]{0,1:T(8,128)}), f32[1024,128]{0,1:T(8,128)}) %all-reduce.25.cloned.1.call-update) | async-done | bytes 524304 | tf_op jit(solution)/shard_map/psum | solution.py:33
  271.8 3.2 fusion.40
  275.1 53.5 %all-reduce.27.cloned.1.call-done = f32[256,128]{0,1:T(8,128)} async-done(((f32[256,128]{0,1:T(8,128)}), f32[256,128]{0,1:T(8,128)}) %all-reduce.27.cloned.1.call-update) | async-done | bytes 131088 | tf_op jit(solution)/shard_map/psum | solution.py:9
  328.6 7.8 fusion.33
  336.4 5.0 fusion.7
  341.4 2.0 copy-done.5
  343.4 0.9 fusion.63
  344.5 38.0 %all-reduce.29.cloned.1.call-done = f32[1024,128]{0,1:T(8,128)} async-done(((f32[1024,128]{0,1:T(8,128)}), f32[1024,128]{0,1:T(8,128)}) %all-reduce.29.cloned.1.call-update) | async-done | bytes 524304 | tf_op jit(solution)/shard_map/psum | solution.py:33
  382.4 3.2 fusion.39
  385.7 0.4 all-reduce.33.cloned.1.call-start
  386.1 53.2 %all-reduce.31.cloned.1.call-done = f32[256,128]{0,1:T(8,128)} async-done(((f32[256,128]{0,1:T(8,128)}), f32[256,128]{0,1:T(8,128)}) %all-reduce.31.cloned.1.call-update) | async-done | bytes 131088 | tf_op jit(solution)/shard_map/psum | solution.py:9
  439.4 7.8 fusion.34
  447.2 5.0 fusion.10
  452.2 1.9 copy-done.9
  454.1 0.9 fusion.62
  455.0 12.3 %fusion.100 = (bf16[1,256,8,1024]{3,2,1,0:T(8,128)(2,1)}, bf16[1,256,8,1024]{3,2,1,0:T(8,128)(2,1)}, bf16[1,256,8,1024]{3,2,1,0:T(8,128)(2,1)}, bf16[1,256,8,1024]{3,2,1,0:T(8,128)(2,1)}) fusion(bf16[4,256,8,1024]{3,2,1,0:T(8,128)(2,1)} %param.14), kind=kLoop, calls=%fused_computation.169 | loop fusion | bytes 33554432 | tf_op jit(solution)/shard_map/slice | solution.py:98
  467.3 25.8 %all-reduce.33.cloned.1.call-done = f32[1024,128]{0,1:T(8,128)} async-done(((f32[1024,128]{0,1:T(8,128)}), f32[1024,128]{0,1:T(8,128)}) %all-reduce.33.cloned.1.call-update) | async-done | bytes 524304 | tf_op jit(solution)/shard_map/psum | solution.py:33
  493.1 2.7 fusion.38
  495.9 54.0 %all-reduce.35.cloned.1.call-done = f32[256,128]{0,1:T(8,128)} async-done(((f32[256,128]{0,1:T(8,128)}), f32[256,128]{0,1:T(8,128)}) %all-reduce.35.cloned.1.call-update) | async-done | bytes 131088 | tf_op jit(solution)/shard_map/psum | solution.py:9
  549.9 7.3 fusion.23
  557.2 7.2 fusion.13
  564.4 1.9 copy-done.13
  566.3 0.9 fusion.61
  567.4 38.0 %all-reduce.37.cloned.1.call-done = f32[1024,128]{0,1:T(8,128)} async-done(((f32[1024,128]{0,1:T(8,128)}), f32[1024,128]{0,1:T(8,128)}) %all-reduce.37.cloned.1.call-update) | async-done | bytes 524304 | tf_op jit(solution)/shard_map/psum | solution.py:33
  605.4 2.7 fusion.37
  608.2 54.0 %all-reduce.39.cloned.1.call-done = f32[256,128]{0,1:T(8,128)} async-done(((f32[256,128]{0,1:T(8,128)}), f32[256,128]{0,1:T(8,128)}) %all-reduce.39.cloned.1.call-update) | async-done | bytes 131088 | tf_op jit(solution)/shard_map/psum | solution.py:9
  662.2 7.3 fusion.25
  669.6 7.2 fusion.16
  676.7 2.0 copy-done.15
  678.7 0.9 fusion.60
  679.9 37.9 %all-reduce.41.cloned.1.call-done = f32[1024,128]{0,1:T(8,128)} async-done(((f32[1024,128]{0,1:T(8,128)}), f32[1024,128]{0,1:T(8,128)}) %all-reduce.41.cloned.1.call-update) | async-done | bytes 524304 | tf_op jit(solution)/shard_map/psum | solution.py:33
  717.8 2.7 fusion.36
  720.5 54.0 %all-reduce.43.cloned.1.call-done = f32[256,128]{0,1:T(8,128)} async-done(((f32[256,128]{0,1:T(8,128)}), f32[256,128]{0,1:T(8,128)}) %all-reduce.43.cloned.1.call-update) | async-done | bytes 131088 | tf_op jit(solution)/shard_map/psum | solution.py:9
  774.5 7.3 fusion.27
  781.9 7.2 fusion.19
  789.1 2.0 copy-done.7
  791.1 0.9 fusion.59
  792.3 37.9 %all-reduce.45.cloned.1.call-done = f32[1024,128]{0,1:T(8,128)} async-done(((f32[1024,128]{0,1:T(8,128)}), f32[1024,128]{0,1:T(8,128)}) %all-reduce.45.cloned.1.call-update) | async-done | bytes 524304 | tf_op jit(solution)/shard_map/psum | solution.py:33
  830.2 2.7 fusion.35
  833.0 54.0 %all-reduce.47.cloned.1.call-done = f32[256,128]{0,1:T(8,128)} async-done(((f32[256,128]{0,1:T(8,128)}), f32[256,128]{0,1:T(8,128)}) %all-reduce.47.cloned.1.call-update) | async-done | bytes 131088 | tf_op jit(solution)/shard_map/psum | solution.py:9
  887.0 7.3 fusion.29
  894.3 8.8 fusion.22
  903.2 1.0 copy.23
  904.2 1.0 copy.24
  905.2 74.3 %reduce-scatter.2.cloned.1.call-done = f32[8,256,128]{1,2,0:T(8,128)} async-done(((f32[8,1024,128]{1,2,0:T(8,128)}), f32[8,256,128]{1,2,0:T(8,128)}) %reduce-scatter.2.cloned.1.call-update) | async-done | bytes 1048592 | tf_op jit(solution)/shard_map/reduce_scatter | solution.py:106
  979.5 1.4 sub.35
  980.8 1.3 copy.25
  (106 shorter events, 2.2 us)
Async XLA Ops:
  7.2 45.0 %all-reduce.17.cloned.1.call-start = ((), (), s32[]{:S(2)}) async-start(), calls=%async_computation.1 | async-start | bytes 1048576 | tf_op jit(solution)/shard_map/psum | solution.py:33
  9.7 41.3 %copy-start.29 = (f32[8,1,4]{0,2,1:T(4,128)S(1)}, f32[8,1,4]{0,2,1:T(4,128)}, u32[]{:S(2)}) copy-start(f32[8,1,4]{0,2,1:T(4,128)} %param.12) | copy-start | bytes 388
  9.7 41.3 %copy-start.27 = (s32[8,1,4]{0,2,1:T(4,128)S(1)}, s32[8,1,4]{0,2,1:T(4,128)}, u32[]{:S(2)}) copy-start(s32[8,1,4]{0,2,1:T(4,128)} %param.11) | copy-start | bytes 388
  9.7 100.9 %all-reduce.19.cloned.1.call-start = ((), (), s32[]{:S(2)}) async-start(), calls=%async_computation.2 | async-start | bytes 262144 | tf_op jit(solution)/shard_map/psum | solution.py:9
  55.4 105.7 %all-reduce.21.cloned.1.call-start = ((), (), s32[]{:S(2)}) async-start(), calls=%async_computation.3 | async-start | bytes 1048576 | tf_op jit(solution)/shard_map/psum | solution.py:33
  110.6 7.9 copy-start.4
  110.6 7.9 copy-start.19
  120.1 2.0 copy-start.17
  123.0 94.9 %all-reduce.23.cloned.1.call-start = ((), (), s32[]{:S(2)}) async-start(), calls=%async_computation.4 | async-start | bytes 262144 | tf_op jit(solution)/shard_map/psum | solution.py:9
  164.4 107.4 %all-reduce.25.cloned.1.call-start = ((), (), s32[]{:S(2)}) async-start(), calls=%async_computation.5 | async-start | bytes 1048576 | tf_op jit(solution)/shard_map/psum | solution.py:33
  217.9 7.8 copy-start.18
  217.9 7.8 copy-start.20
  230.7 2.0 copy-start.11
  233.6 95.0 %all-reduce.27.cloned.1.call-start = ((), (), s32[]{:S(2)}) async-start(), calls=%async_computation.6 | async-start | bytes 262144 | tf_op jit(solution)/shard_map/psum | solution.py:9
  275.0 107.4 %all-reduce.29.cloned.1.call-start = ((), (), s32[]{:S(2)}) async-start(), calls=%async_computation.7 | async-start | bytes 1048576 | tf_op jit(solution)/shard_map/psum | solution.py:33
  328.6 7.8 copy-start.12
  328.6 7.8 copy-start.21
  336.4 7.9 copy-start.30
  336.4 7.9 copy-start.28
  341.4 2.0 copy-start.5
  344.3 95.1 %all-reduce.31.cloned.1.call-start = ((), (), s32[]{:S(2)}) async-start(), calls=%async_computation.8 | async-start | bytes 262144 | tf_op jit(solution)/shard_map/psum | solution.py:9
  385.7 107.4 %all-reduce.33.cloned.1.call-start = ((), (), s32[]{:S(2)}) async-start(), calls=%async_computation.9 | async-start | bytes 1048576 | tf_op jit(solution)/shard_map/psum | solution.py:33
  439.4 7.8 copy-start.6
  439.4 7.8 copy-start.22
  452.2 1.9 copy-start.9
  455.0 94.9 %all-reduce.35.cloned.1.call-start = ((), (), s32[]{:S(2)}) async-start(), calls=%async_computation.10 | async-start | bytes 262144 | tf_op jit(solution)/shard_map/psum | solution.py:9
  495.8 109.6 %all-reduce.37.cloned.1.call-start = ((), (), s32[]{:S(2)}) async-start(), calls=%async_computation.11 | async-start | bytes 1048576 | tf_op jit(solution)/shard_map/psum | solution.py:33
  549.9 7.3 copy-start.3
  549.9 7.3 copy-start.10
  549.9 7.3 copy-start.23
  564.4 1.9 copy-start.13
  567.2 95.0 %all-reduce.39.cloned.1.call-start = ((), (), s32[]{:S(2)}) async-start(), calls=%async_computation.12 | async-start | bytes 262144 | tf_op jit(solution)/shard_map/psum | solution.py:9
  608.1 109.6 %all-reduce.41.cloned.1.call-start = ((), (), s32[]{:S(2)}) async-start(), calls=%async_computation.13 | async-start | bytes 1048576 | tf_op jit(solution)/shard_map/psum | solution.py:33
  662.2 7.3 copy-start.2
  662.2 7.3 copy-start.14
  662.2 7.3 copy-start.24
  676.7 2.0 copy-start.15
  679.6 94.9 %all-reduce.43.cloned.1.call-start = ((), (), s32[]{:S(2)}) async-start(), calls=%async_computation.14 | async-start | bytes 262144 | tf_op jit(solution)/shard_map/psum | solution.py:9
  720.5 109.7 %all-reduce.45.cloned.1.call-start = ((), (), s32[]{:S(2)}) async-start(), calls=%async_computation.15 | async-start | bytes 1048576 | tf_op jit(solution)/shard_map/psum | solution.py:33
  774.5 7.3 copy-start.1
  774.5 7.3 copy-start.16
  774.5 7.3 copy-start.25
  789.1 2.0 copy-start.7
  792.0 95.0 %all-reduce.47.cloned.1.call-start = ((), (), s32[]{:S(2)}) async-start(), calls=%async_computation.16 | async-start | bytes 262144 | tf_op jit(solution)/shard_map/psum | solution.py:9
  832.9 146.6 %reduce-scatter.2.cloned.1.call-start = ((), (), s32[]{:S(2)}) async-start(), calls=%async_computation.17 | async-start | bytes 5242880 | tf_op jit(solution)/shard_map/reduce_scatter | solution.py:106
  887.0 7.3 copy-start
  887.0 7.3 copy-start.8
  887.0 7.3 copy-start.26
Sparse Core Ops, SparseCore 0:
  10.9 41.2 all-reduce.16
  55.8 54.7 all-reduce.18
  123.1 37.9 all-reduce.20
  164.6 53.2 all-reduce.22
  233.7 38.0 all-reduce.24
  275.3 53.2 all-reduce.26
  344.4 37.9 all-reduce.28
  386.0 53.2 all-reduce.30
  455.1 37.9 all-reduce.32
  496.6 53.2 all-reduce.34
  567.3 38.0 all-reduce.36
  608.9 53.2 all-reduce.38
  679.7 37.9 all-reduce.40
  721.2 53.2 all-reduce.42
  792.1 38.0 all-reduce.44
  833.6 53.2 all-reduce.46
  903.2 76.1 reduce-scatter.1
where the time goes:
time: 996 us; the launch traced here: 989 us
  waiting for transfers between devices  761 us (76%)
  matrix products  131 us (13%)
  local copies, waits for them, and re-layouts  72.4 us (7%)
  between operations  15 us (2%)
    psum x8, waiting for transfers between devices, from_root(): return lax.psum(block, axis)  431 us
    psum x8, waiting for transfers between devices, solve_tile(): summed = lax.psum(partial_value - placed, 'col')  255 us
    reduce_scatter x1, waiting for transfers between devices, on_device(): summed = lax.psum_scatter(updates, 'col', scatter_dimension=1, tiled=True)  74.3 us
    dot_general x8, matrix products, tile_terms(): jnp.einsum(form, stored.astype(jnp.float32), solved, precision=lax.Precis...  61.5 us
    dot_general x8, matrix products, tile_terms(): jnp.einsum(form, stored, short_piece, preferred_element_type=jnp.float32)  45.7 us
    slice x1, local copies, waits for them, and re-layouts, on_device(): factor_head[:, :, step, :]  41.2 us
  transfers between devices with their start and end apart: 17, of which 17 were waited for; matrix products, arithmetic and copies ran while one was open for 6% of the time, Pallas kernels for 0%

commit v1 on v0

--- a/solution.py
+++ b/solution.py
@@ -30,7 +30,9 @@
         lax.axis_index("col") * share_rows,
         0,
     )
-    summed = lax.psum(partial_value - placed, "col")
+    block_2 = partial_value - placed
+    parts = lax.all_gather(block_2, "col", axis=0, tiled=False)
+    summed = parts.sum(axis=0)
     solved = invert(-summed)
     return from_root(solved, "row", owner_row)
 

time: 996 us -> 1070 us (1.074)
  waiting for transfers between devices: 761 us -> 799 us
  local copies, waits for them, and re-layouts: 72.4 us -> 97.4 us
  other arithmetic: 8.37 us -> 19.5 us
    all_gather x0 -> x8, waiting for transfers between devices: none -> 307 us  [solve_tile(): parts = lax.all_gather(block_2, 'col', axis=0, tiled=False)]
    psum x8 -> x0, waiting for transfers between devices: 255 us -> none  [solve_tile(): summed = lax.psum(partial_value - placed, 'col')]
    all_gather x0 -> x8, local copies, waits for them, and re-layouts: none -> 21.4 us  [solve_tile(): parts = lax.all_gather(block_2, 'col', axis=0, tiled=False)]
    psum x8, waiting for transfers between devices: 431 us -> 418 us  [from_root(): return lax.psum(block, axis)]
where the time goes in v1:
time: 1070 us; the launch traced here: 1060 us
  waiting for transfers between devices  799 us (75%)
  matrix products  130 us (12%)
  local copies, waits for them, and re-layouts  97.4 us (9%)
  other arithmetic  19.5 us (2%)
  between operations  15.2 us (1%)
    psum x8, waiting for transfers between devices, from_root(): return lax.psum(block, axis)  418 us
    all_gather x8, waiting for transfers between devices, solve_tile(): parts = lax.all_gather(block_2, 'col', axis=0, tiled=False)  307 us
    reduce_scatter x1, waiting for transfers between devices, on_device(): summed = lax.psum_scatter(updates, 'col', scatter_dimension=1, tiled=True)  73.4 us
    dot_general x8, matrix products, tile_terms(): jnp.einsum(form, stored.astype(jnp.float32), solved, precision=lax.Precis...  61.5 us
    dot_general x8, matrix products, tile_terms(): jnp.einsum(form, stored, short_piece, preferred_element_type=jnp.float32)  45.7 us
    slice x1, local copies, waits for them, and re-layouts, on_device(): factor_head[:, :, step, :]  41.4 us
  transfers between devices with their start and end apart: 17, of which 17 were waited for; matrix products, arithmetic and copies ran while one was open for 6% of the time, Pallas kernels for 0%

profile of v1, /device:TPU:0, one launch (start us, length us, event | category | flops | bytes accessed | tf_op | source)
XLA Modules:
  0.0 1062.9 jit_solution(10592684906575062649)
XLA Ops:
  7.2 1.6 copy.26
  10.5 41.4 %fusion.101 = (bf16[8,1024,1,256]{3,2,1,0:T(2,128)(2,1)}, bf16[8,1024,1,256]{3,2,1,0:T(2,128)(2,1)}, bf16[8,1024,1,256]{3,2,1,0:T(2,128)(2,1)}, bf16[8,1024,1,256]{3,2,1,0:T(2,128)(2,1)}) fusion(bf16[8,1024,4,256]{3,2,1,0:T(4,128)(2,1)} %param.10), kind=kLoop, calls=%fused_computation.170 | loop fusion | bytes 33554432 | tf_op jit(solution)/shard_map/slice | solution.py:74
  51.9 6.6 all-gather.17.cloned.1.call-done
  58.5 2.7 reshape.109
  61.2 1.3 reduce_sum.72
  62.5 3.1 fusion.42
  65.7 52.4 %all-reduce.9.cloned.1.call-done = f32[256,128]{0,1:T(8,128)} async-done(((f32[256,128]{0,1:T(8,128)}), f32[256,128]{0,1:T(8,128)}) %all-reduce.9.cloned.1.call-update) | async-done | bytes 131088 | tf_op jit(solution)/shard_map/psum | solution.py:9
  118.0 7.9 fusion.31
  126.0 1.5 fusion.1
  127.5 2.0 copy-done.17
  130.7 44.9 %all-gather.19.cloned.1.call-done = f32[4096,128]{0,1:T(8,128)} async-done(((f32[1024,128]{0,1:T(8,128)}), f32[4096,128]{0,1:T(8,128)}) %all-gather.19.cloned.1.call-update) | async-done | bytes 2097168 | tf_op jit(solution)/shard_map/all_gather | solution.py:34
  175.7 2.7 reshape.110
  178.3 1.3 reduce_sum.73
  179.7 3.1 fusion.41
  182.8 52.4 %all-reduce.11.cloned.1.call-done = f32[256,128]{0,1:T(8,128)} async-done(((f32[256,128]{0,1:T(8,128)}), f32[256,128]{0,1:T(8,128)}) %all-reduce.11.cloned.1.call-update) | async-done | bytes 131088 | tf_op jit(solution)/shard_map/psum | solution.py:9
  235.2 7.8 fusion.32
  243.0 5.0 fusion.4
  248.0 2.0 copy-done.11
  250.9 45.1 %all-gather.21.cloned.1.call-done = f32[4096,128]{0,1:T(8,128)} async-done(((f32[1024,128]{0,1:T(8,128)}), f32[4096,128]{0,1:T(8,128)}) %all-gather.21.cloned.1.call-update) | async-done | bytes 2097168 | tf_op jit(solution)/shard_map/all_gather | solution.py:34
  296.0 2.7 reshape.111
  300.0 3.1 fusion.40
  303.6 51.9 %all-reduce.13.cloned.1.call-done = f32[256,128]{0,1:T(8,128)} async-done(((f32[256,128]{0,1:T(8,128)}), f32[256,128]{0,1:T(8,128)}) %all-reduce.13.cloned.1.call-update) | async-done | bytes 131088 | tf_op jit(solution)/shard_map/psum | solution.py:9
  355.5 7.8 fusion.33
  363.3 5.0 fusion.7
  368.3 2.0 copy-done.7
  372.3 44.2 %all-gather.23.cloned.1.call-done = f32[4096,128]{0,1:T(8,128)} async-done(((f32[1024,128]{0,1:T(8,128)}), f32[4096,128]{0,1:T(8,128)}) %all-gather.23.cloned.1.call-update) | async-done | bytes 2097168 | tf_op jit(solution)/shard_map/all_gather | solution.py:34
  416.4 2.7 reshape.112
  419.1 1.3 reduce_sum.75
  420.4 3.1 fusion.39
  423.7 52.2 %all-reduce.15.cloned.1.call-done = f32[256,128]{0,1:T(8,128)} async-done(((f32[256,128]{0,1:T(8,128)}), f32[256,128]{0,1:T(8,128)}) %all-reduce.15.cloned.1.call-update) | async-done | bytes 131088 | tf_op jit(solution)/shard_map/psum | solution.py:9
  475.9 7.8 fusion.34
  483.8 5.0 fusion.10
  488.8 2.0 copy-done.5
  493.0 12.5 %fusion.100 = (bf16[1,256,8,1024]{3,2,1,0:T(8,128)(2,1)}, bf16[1,256,8,1024]{3,2,1,0:T(8,128)(2,1)}, bf16[1,256,8,1024]{3,2,1,0:T(8,128)(2,1)}, bf16[1,256,8,1024]{3,2,1,0:T(8,128)(2,1)}) fusion(bf16[4,256,8,1024]{3,2,1,0:T(8,128)(2,1)} %param.14), kind=kLoop, calls=%fused_computation.169 | loop fusion | bytes 33554432 | tf_op jit(solution)/shard_map/slice | solution.py:100
  505.4 31.5 %all-gather.25.cloned.1.call-done = f32[4096,128]{0,1:T(8,128)} async-done(((f32[1024,128]{0,1:T(8,128)}), f32[4096,128]{0,1:T(8,128)}) %all-gather.25.cloned.1.call-update) | async-done | bytes 2097168 | tf_op jit(solution)/shard_map/all_gather | solution.py:34
  536.9 2.7 reshape.113
  540.9 2.5 fusion.38
  543.7 52.1 %all-reduce.17.cloned.1.call-done = f32[256,128]{0,1:T(8,128)} async-done(((f32[256,128]{0,1:T(8,128)}), f32[256,128]{0,1:T(8,128)}) %all-reduce.17.cloned.1.call-update) | async-done | bytes 131088 | tf_op jit(solution)/shard_map/psum | solution.py:9
  595.9 7.3 fusion.23
  603.3 7.2 fusion.13
  610.4 2.0 copy-done.13
  613.9 44.7 %all-gather.27.cloned.1.call-done = f32[4096,128]{0,1:T(8,128)} async-done(((f32[1024,128]{0,1:T(8,128)}), f32[4096,128]{0,1:T(8,128)}) %all-gather.27.cloned.1.call-update) | async-done | bytes 2097168 | tf_op jit(solution)/shard_map/all_gather | solution.py:34
  658.6 2.7 reshape.114
  662.6 2.5 fusion.37
  665.2 52.4 %all-reduce.19.cloned.1.call-done = f32[256,128]{0,1:T(8,128)} async-done(((f32[256,128]{0,1:T(8,128)}), f32[256,128]{0,1:T(8,128)}) %all-reduce.19.cloned.1.call-update) | async-done | bytes 131088 | tf_op jit(solution)/shard_map/psum | solution.py:9
  717.6 7.3 fusion.25
  724.9 7.1 fusion.16
  732.1 2.0 copy-done.15
  735.3 45.0 %all-gather.29.cloned.1.call-done = f32[4096,128]{0,1:T(8,128)} async-done(((f32[1024,128]{0,1:T(8,128)}), f32[4096,128]{0,1:T(8,128)}) %all-gather.29.cloned.1.call-update) | async-done | bytes 2097168 | tf_op jit(solution)/shard_map/all_gather | solution.py:34
  780.2 2.7 reshape.115
  784.2 2.5 fusion.36
  786.9 52.4 %all-reduce.21.cloned.1.call-done = f32[256,128]{0,1:T(8,128)} async-done(((f32[256,128]{0,1:T(8,128)}), f32[256,128]{0,1:T(8,128)}) %all-reduce.21.cloned.1.call-update) | async-done | bytes 131088 | tf_op jit(solution)/shard_map/psum | solution.py:9
  839.2 7.3 fusion.27
  846.6 7.2 fusion.19
  853.7 2.0 copy-done.9
  856.9 44.9 %all-gather.31.cloned.1.call-done = f32[4096,128]{0,1:T(8,128)} async-done(((f32[1024,128]{0,1:T(8,128)}), f32[4096,128]{0,1:T(8,128)}) %all-gather.31.cloned.1.call-update) | async-done | bytes 2097168 | tf_op jit(solution)/shard_map/all_gather | solution.py:34
  901.9 2.7 reshape.116
  905.8 2.5 fusion.35
  908.5 52.4 %all-reduce.23.cloned.1.call-done = f32[256,128]{0,1:T(8,128)} async-done(((f32[256,128]{0,1:T(8,128)}), f32[256,128]{0,1:T(8,128)}) %all-reduce.23.cloned.1.call-update) | async-done | bytes 131088 | tf_op jit(solution)/shard_map/psum | solution.py:9
  960.8 7.3 fusion.29
  968.2 8.8 fusion.22
  979.9 73.4 %reduce-scatter.2.cloned.1.call-done = f32[8,256,128]{1,2,0:T(8,128)} async-done(((f32[8,1024,128]{1,2,0:T(8,128)}), f32[8,256,128]{1,2,0:T(8,128)}) %reduce-scatter.2.cloned.1.call-update) | async-done | bytes 1048592 | tf_op jit(solution)/shard_map/reduce_scatter | solution.py:108
  1053.3 1.4 sub.35
  1054.7 1.3 copy.39
  (152 shorter events, 22.3 us)
Async XLA Ops:
  7.2 2.8 copy-start.42
  7.2 2.8 copy-start.44
  7.2 51.4 %all-gather.17.cloned.1.call-start = ((), (), s32[]{:S(2)}) async-start(), calls=%async_computation.10 | async-start | bytes 2621440 | tf_op jit(solution)/shard_map/all_gather | solution.py:34
  8.8 43.1 %copy-start.19 = (f32[8,256,128]{1,2,0:T(8,128)}, f32[8,256,128]{1,2,0:T(8,128)S(1)}, u32[]{:S(2)}) copy-start(f32[8,256,128]{1,2,0:T(8,128)S(1)} %copy.26) | copy-start | bytes 3145732
  9.9 108.1 %all-reduce.9.cloned.1.call-start = ((), (), s32[]{:S(2)}) async-start(), calls=%async_computation.1 | async-start | bytes 262144 | tf_op jit(solution)/shard_map/psum | solution.py:9
  65.6 110.0 %all-gather.19.cloned.1.call-start = ((), (), s32[]{:S(2)}) async-start(), calls=%async_computation.11 | async-start | bytes 2621440 | tf_op jit(solution)/shard_map/all_gather | solution.py:34
  118.0 7.9 copy-start.4
  118.0 7.9 copy-start.21
  127.5 2.1 copy-start.17
  130.5 104.7 %all-reduce.11.cloned.1.call-start = ((), (), s32[]{:S(2)}) async-start(), calls=%async_computation.2 | async-start | bytes 262144 | tf_op jit(solution)/shard_map/psum | solution.py:9
  182.7 113.3 %all-gather.21.cloned.1.call-start = ((), (), s32[]{:S(2)}) async-start(), calls=%async_computation.12 | async-start | bytes 2621440 | tf_op jit(solution)/shard_map/all_gather | solution.py:34
  235.2 7.8 copy-start.18
  235.2 7.8 copy-start.22
  248.0 2.0 copy-start.11
  250.8 104.7 %all-reduce.13.cloned.1.call-start = ((), (), s32[]{:S(2)}) async-start(), calls=%async_computation.3 | async-start | bytes 262144 | tf_op jit(solution)/shard_map/psum | solution.py:9
  303.1 113.3 %all-gather.23.cloned.1.call-start = ((), (), s32[]{:S(2)}) async-start(), calls=%async_computation.13 | async-start | bytes 2621440 | tf_op jit(solution)/shard_map/all_gather | solution.py:34
  355.5 7.8 copy-start.12
  355.5 7.8 copy-start.23
  355.5 7.8 copy-start.39
  368.3 2.1 copy-start.7
  371.2 104.7 %all-reduce.15.cloned.1.call-start = ((), (), s32[]{:S(2)}) async-start(), calls=%async_computation.4 | async-start | bytes 262144 | tf_op jit(solution)/shard_map/psum | solution.py:9
  423.5 113.4 %all-gather.25.cloned.1.call-start = ((), (), s32[]{:S(2)}) async-start(), calls=%async_computation.14 | async-start | bytes 2621440 | tf_op jit(solution)/shard_map/all_gather | solution.py:34
  475.9 7.8 copy-start.8
  475.9 7.8 copy-start.24
  475.9 7.8 copy-start.37
  483.8 8.0 copy-start.45
  483.8 8.6 copy-start.43
  488.8 2.1 copy-start.5
  491.7 104.2 %all-reduce.17.cloned.1.call-start = ((), (), s32[]{:S(2)}) async-start(), calls=%async_computation.5 | async-start | bytes 262144 | tf_op jit(solution)/shard_map/psum | solution.py:9
  543.4 115.1 %all-gather.27.cloned.1.call-start = ((), (), s32[]{:S(2)}) async-start(), calls=%async_computation.15 | async-start | bytes 2621440 | tf_op jit(solution)/shard_map/all_gather | solution.py:34
  595.9 7.3 copy-start.3
  595.9 7.4 copy-start.6
  595.9 7.4 copy-start.26
  595.9 7.4 copy-start.34
  595.9 7.4 copy-start.35
  595.9 7.4 copy-start.41
  610.4 2.1 copy-start.13
  613.4 104.2 %all-reduce.19.cloned.1.call-start = ((), (), s32[]{:S(2)}) async-start(), calls=%async_computation.6 | async-start | bytes 262144 | tf_op jit(solution)/shard_map/psum | solution.py:9
  665.1 115.1 %all-gather.29.cloned.1.call-start = ((), (), s32[]{:S(2)}) async-start(), calls=%async_computation.16 | async-start | bytes 2621440 | tf_op jit(solution)/shard_map/all_gather | solution.py:34
  717.5 7.4 copy-start.2
  717.5 7.4 copy-start.14
  717.5 7.4 copy-start.28
  717.5 7.4 copy-start.32
  717.5 7.4 copy-start.33
  717.5 7.4 copy-start.40
  732.1 2.1 copy-start.15
  735.0 104.2 %all-reduce.21.cloned.1.call-start = ((), (), s32[]{:S(2)}) async-start(), calls=%async_computation.7 | async-start | bytes 262144 | tf_op jit(solution)/shard_map/psum | solution.py:9
  786.8 115.1 %all-gather.31.cloned.1.call-start = ((), (), s32[]{:S(2)}) async-start(), calls=%async_computation.17 | async-start | bytes 2621440 | tf_op jit(solution)/shard_map/all_gather | solution.py:34
  839.2 7.3 copy-start.1
  839.2 7.3 copy-start.16
  839.2 7.3 copy-start.30
  839.2 7.4 copy-start.38
  853.7 2.0 copy-start.9
  856.7 104.2 %all-reduce.23.cloned.1.call-start = ((), (), s32[]{:S(2)}) async-start(), calls=%async_computation.8 | async-start | bytes 262144 | tf_op jit(solution)/shard_map/psum | solution.py:9
  908.4 144.9 %reduce-scatter.2.cloned.1.call-start = ((), (), s32[]{:S(2)}) async-start(), calls=%async_computation.9 | async-start | bytes 5242880 | tf_op jit(solution)/shard_map/reduce_scatter | solution.py:108
  960.8 7.3 copy-start
  960.8 7.3 copy-start.10
  960.8 7.4 copy-start.31
  960.8 7.4 copy-start.36
  977.0 0.9 copy-start.25
  977.0 1.9 copy-start.27
  977.0 1.9 copy-start.29
  977.0 76.4 %copy-start.20 = (f32[8,256,128]{1,2,0:T(8,128)S(1)}, f32[8,256,128]{1,2,0:T(8,128)}, u32[]{:S(2)}) copy-start(f32[8,256,128]{1,2,0:T(8,128)} %copy-done.19) | copy-start | bytes 3145732
Sparse Core Ops, SparseCore 0:
  10.1 48.3 all-gather.16
  65.8 52.2 all-reduce.8
  130.6 45.0 all-gather.18
  182.9 52.2 all-reduce.10
  250.9 45.0 all-gather.20
  303.2 52.2 all-reduce.12
  371.3 45.0 all-gather.22
  423.6 52.2 all-reduce.14
  491.8 45.0 all-gather.24
  543.6 52.2 all-reduce.16
  613.5 45.0 all-gather.26
  665.2 52.2 all-reduce.18
  735.2 45.0 all-gather.28
  786.9 52.2 all-reduce.20
  856.8 45.0 all-gather.30
  908.5 52.2 all-reduce.22
  977.1 76.1 reduce-scatter.1
